TPU v7x, 32 devices: a whole 2x2x4 slice. The times are simulated.
32 devices in a mesh: rows: 8 (over y, x, core), hub: 4 (over z).
Axes of the slice: x: 2, y: 2, z: 4, core: 2. Of those that a mesh axis runs over, the one named last changes fastest.
Arguments:
- tail_blocks: float32 [2304, 128, 128], P(('rows', 'hub')), may hold values from -0.21875 to 0.21875
- tail_row: int32 [2304], P(('rows', 'hub')), may hold values from 0 to 15
- tail_owner: int32 [2304, 1], P(('rows', 'hub')), may hold values from 0 to 7; in each aligned block of 72 rows (0 to 71, 72 to 143, ...) at most 27 rows name the same one
- tail_slot: int32 [2304], P(('rows', 'hub')), may hold values from 0 to 63
- hub_blocks: float32 [768, 128, 128], P(('rows', 'hub')), may hold values from -0.21875 to 0.21875
- hub_row: int32 [768], P(('rows', 'hub')), may hold values from 0 to 15
- hub_col: int32 [768], P(('rows', 'hub')), may hold values from 0 to 127
- x_tail: float32 [2048, 128], P(('rows', 'hub')), may hold values from 0 to 0.5
- cost_tail: float32 [2048, 128], P(('rows', 'hub')), may hold values from -6 to 6
- upper_tail: float32 [2048, 128], P(('rows', 'hub')), may hold values from 0.5 to 2
- x_hub: float32 [128, 128], P('hub'), may hold values from 0 to 0.5
- cost_hub: float32 [128, 128], P('hub'), may hold values from -6 to 6
- upper_hub: float32 [128, 128], P('hub'), may hold values from 0.5 to 2
- duals: float32 [512, 128], P(('rows', 'hub')), may hold values from 0 to 1
- demand: float32 [512, 128], P(('rows', 'hub')), may hold values from -6 to 6
Outputs:
- x_tail_out: float32 [2048, 128], P(('rows', 'hub'))
- x_hub_out: float32 [128, 128], P('hub')
- duals_out: float32 [512, 128], P(('rows', 'hub'))
Inputs may be any that keep to these rules, and one draw needn't show every extreme that they name: `tail_owner`: among the blocks of one device no owner is named more than 27 times; on some device one owner is named exactly 27 times.
All inputs are finite; a program needn't handle non-finite values.
Results may differ from a plain program's by a relative error of at most 0.0001.
Values sent between devices are 32-bit elements; how exact they have to be, the bound alone decides.
No kernel may reach another device: no remote copies, remote signals or barrier semaphores. Data moves between devices by JAX's collectives and lax.ppermute only.
A program may use at most 64 MiB of HBM per device.

v0:
```python
import jax
import jax.numpy as jnp
from jax import lax
from jax.sharding import PartitionSpec as P

ITERS = 3
primal_step = 0.25
dual_step = 0.25


def on_device(
    tail_blocks,
    tail_row,
    tail_owner,
    tail_slot,
    hub_blocks,
    hub_row,
    hub_col,
    x_tail,
    cost_tail,
    upper_tail,
    x_hub,
    cost_hub,
    upper_hub,
    duals,
    demand,
):
    highest = lax.Precision.HIGHEST
    row_devs = lax.axis_size("rows")
    hub_devs = lax.axis_size("hub")
    tail_count = tail_blocks.shape[0]
    col_blocks = x_tail.shape[0]
    row_blocks = duals.shape[0]
    hub_share = x_hub.shape[0]
    hub_total = hub_share * hub_devs
    width = x_tail.shape[1]
    capacity = max(2, 3 * tail_count // row_devs)
    owners = tail_owner[:, 0]
    hits = (owners[:, None] == jnp.arange(row_devs, dtype=jnp.int32)[None, :]).astype(jnp.int32)
    within = jnp.sum(jnp.cumsum(hits, axis=0) * hits, axis=1) - 1
    places = owners * capacity + within
    asked_slots = jnp.zeros((row_devs * capacity,), jnp.int32).at[places].set(tail_slot)
    requested = lax.all_to_all(
        asked_slots.reshape(row_devs, capacity), "rows", split_axis=0, concat_axis=0, tiled=True
    ).reshape(-1)
    collector = (jnp.arange(col_blocks, dtype=jnp.int32)[:, None] == requested[None, :]).astype(
        jnp.float32
    )
    tail_rowpick = (jnp.arange(row_blocks, dtype=jnp.int32)[:, None] == tail_row[None, :]).astype(
        jnp.float32
    )
    hub_rowpick = (jnp.arange(row_blocks, dtype=jnp.int32)[:, None] == hub_row[None, :]).astype(
        jnp.float32
    )
    hub_state = x_hub
    hub_pick = (jnp.arange(hub_total, dtype=jnp.int32)[:, None] == hub_col[None, :]).astype(
        jnp.float32
    )
    tail_state = x_tail
    for iteration in range(ITERS):
        tail_terms = jnp.einsum("bij,bi->bj", tail_blocks, duals[tail_row], precision=highest)
        outgoing = jnp.zeros((row_devs * capacity, width), jnp.float32).at[places].set(tail_terms)
        arrived = lax.all_to_all(
            outgoing.reshape(row_devs, capacity, width),
            "rows",
            split_axis=0,
            concat_axis=0,
            tiled=True,
        )
        tail_image = jnp.dot(
            collector,
            arrived.reshape(-1, width),
            precision=highest,
            preferred_element_type=jnp.float32,
        )
        tail_next = jnp.minimum(
            jnp.maximum(tail_state - primal_step * (cost_tail - tail_image), 0.0), upper_tail
        )
        tail_extra = 2.0 * tail_next - tail_state
        hub_terms = jnp.einsum("bij,bi->bj", hub_blocks, duals[hub_row], precision=highest)
        hub_partial = jnp.dot(
            hub_pick, hub_terms, precision=highest, preferred_element_type=jnp.float32
        )
        hub_sums = lax.psum_scatter(hub_partial, "hub", scatter_dimension=0, tiled=True)
        hub_sums = lax.psum(hub_sums, "rows")
        hub_next = jnp.minimum(
            jnp.maximum(hub_state - primal_step * (cost_hub - hub_sums), 0.0), upper_hub
        )
        hub_extra = 2.0 * hub_next - hub_state
        hub_full = lax.all_gather(hub_extra, "hub", axis=0, tiled=True)
        gathered = lax.all_gather(tail_extra, "rows", axis=0, tiled=True)
        tail_picked = gathered[owners * col_blocks + tail_slot]
        tail_product = jnp.einsum("bij,bj->bi", tail_blocks, tail_picked, precision=highest)
        hub_product = jnp.einsum("bij,bj->bi", hub_blocks, hub_full[hub_col], precision=highest)
        primal_image = jnp.dot(
            tail_rowpick, tail_product, precision=highest, preferred_element_type=jnp.float32
        )
        primal_image = primal_image + jnp.dot(
            hub_rowpick, hub_product, precision=highest, preferred_element_type=jnp.float32
        )
        duals = jnp.maximum(duals + dual_step * (demand - primal_image), 0.0)
        tail_state = tail_next
        hub_state = hub_next
    return (tail_state, hub_state, duals)


def solution(mesh):
    in_specs = (
        P(("rows", "hub"), None, None),
        P(("rows", "hub")),
        P(("rows", "hub"), None),
        P(("rows", "hub")),
        P(("rows", "hub"), None, None),
        P(("rows", "hub")),
        P(("rows", "hub")),
        P(("rows", "hub"), None),
        P(("rows", "hub"), None),
        P(("rows", "hub"), None),
        P("hub", None),
        P("hub", None),
        P("hub", None),
        P(("rows", "hub"), None),
        P(("rows", "hub"), None),
    )
    out_specs = (P(("rows", "hub"), None), P("hub", None), P(("rows", "hub"), None))
    return jax.shard_map(
        on_device, mesh=mesh, in_specs=in_specs, out_specs=out_specs, check_vma=False
    )
```

profile of v0, /device:TPU:0, one launch (start us, length us, event | category | flops | bytes accessed | tf_op | source)
XLA Modules:
  0.0 261.1 jit_solution(8980955782605521598)
XLA Ops:
  9.7 0.9 scatter_custom_fusion
  11.3 5.2 %all-to-all-start = ((s32[8,1,27]{2,1,0:T(1,128)}), s32[8,1,27]{2,1,0:T(1,128)S(1)}, u32[]{:S(2)}, u32[]{:S(2)}) async-start(s32[8,1,27]{2,1,0:T(1,128)} %all_to_all.15), calls=%async_computation | async-start | bytes 8192 | tf_op jit(solution)/shard_map/all_to_all | solution.py:43
  17.2 1.3 gather_fusion.2
  18.5 1.4 fusion.54
  19.9 1.5 fusion.26
  23.4 1.3 gather_fusion
  24.7 5.8 %fusion.52 = f32[72,1,128]{2,1,0:T(1,128)S(1)} fusion(f32[72,128,1]{1,2,0:T(1,128)S(1)} %bitcast.112, f32[72,128,128]{2,1,0:T(8,128)} %param.15), kind=kOutput, calls=%fused_computation.99 | convolution fusion | flops 14155776 | bytes 4792320 | tf_op jit(solution)/shard_map/bij,bi->bj/dot_general | solution.py:61
  32.0 4.2 %all-to-all-start.1 = ((f32[8,27,128]{2,1,0:T(8,128)}), f32[8,27,128]{2,1,0:T(8,128)S(1)}, u32[]{:S(2)}, u32[]{:S(2)}) async-start(f32[8,27,128]{2,1,0:T(8,128)} %reshape.42), calls=%async_computation.1 | async-start | bytes 262144 | tf_op jit(solution)/shard_map/all_to_all | solution.py:63
  37.4 4.2 %all-to-all-done.1 = f32[8,27,128]{2,1,0:T(8,128)S(1)} async-done(((f32[8,27,128]{2,1,0:T(8,128)}), f32[8,27,128]{2,1,0:T(8,128)S(1)}, u32[]{:S(2)}, u32[]{:S(2)}) %all-to-all-start.1) | async-done | bytes 110624 | tf_op jit(solution)/shard_map/all_to_all | solution.py:63
  41.9 8.4 %all_gather.18 = f32[512,128]{1,0:T(8,128)S(1)} all-gather(f32[64,128]{1,0:T(8,128)S(1)} %get-tuple-element.9), channel_id=1, replica_groups=mesh['rows'=8,'hub'=4] {'rows'}, dimensions={0}, use_global_device_ids=true | all-gather | bytes 294912 | tf_op jit(solution)/shard_map/all_gather | solution.py:91
  50.9 9.2 %fusion.53 = f32[72,1,128]{2,1,0:T(1,128)S(1)} fusion(f32[72,128,1]{1,2,0:T(1,128)S(1)} %bitcast.109, f32[72,128,128]{2,1,0:T(8,128)} %param.15), kind=kOutput, calls=%fused_computation.100 | convolution fusion | flops 14155776 | bytes 4792320 | tf_op jit(solution)/shard_map/bij,bj->bi/dot_general | solution.py:93
  60.2 23.7 %psum.21 = f32[32,128]{1,0:T(8,128)S(1)} all-reduce(f32[32,128]{1,0:T(8,128)} %reduce-scatter.4.cloned.1.call-done), channel_id=1, replica_groups=mesh['rows'=8,'hub'=4] {'rows'}, use_global_device_ids=true, to_apply=%region_5.6 | all-reduce | flops 4096 | bytes 32768 | tf_op jit(solution)/shard_map/psum | solution.py:85
  84.0 13.6 %all_gather.19 = f32[128,128]{1,0:T(8,128)S(1)} all-gather(f32[32,128]{1,0:T(8,128)S(1)} %get-tuple-element.7), channel_id=1, replica_groups=mesh['rows'=8,'hub'=4] {'hub'}, dimensions={0}, use_global_device_ids=true | all-gather | bytes 81920 | tf_op jit(solution)/shard_map/all_gather | solution.py:90
  98.1 2.5 fusion.55
  102.0 5.8 %fusion.56 = f32[72,1,128]{2,1,0:T(1,128)S(1)} fusion(f32[72,128,1]{1,2,0:T(1,128)S(1)} %bitcast.110, f32[72,128,128]{2,1,0:T(8,128)} %param.15), kind=kOutput, calls=%fused_computation.103 | convolution fusion | flops 14155776 | bytes 4792320 | tf_op jit(solution)/shard_map/bij,bi->bj/dot_general | solution.py:61
  109.2 3.4 %all-to-all-start.2 = ((f32[8,27,128]{2,1,0:T(8,128)}), f32[8,27,128]{2,1,0:T(8,128)S(1)}, u32[]{:S(2)}, u32[]{:S(2)}) async-start(f32[8,27,128]{2,1,0:T(8,128)} %reshape.44), calls=%async_computation.3 | async-start | bytes 262144 | tf_op jit(solution)/shard_map/all_to_all | solution.py:63
  112.7 1.4 fusion.58
  115.0 3.2 %all-to-all-done.2 = f32[8,27,128]{2,1,0:T(8,128)S(1)} async-done(((f32[8,27,128]{2,1,0:T(8,128)}), f32[8,27,128]{2,1,0:T(8,128)S(1)}, u32[]{:S(2)}, u32[]{:S(2)}) %all-to-all-start.2) | async-done | bytes 110624 | tf_op jit(solution)/shard_map/all_to_all | solution.py:63
  118.4 8.4 %all_gather.20 = f32[512,128]{1,0:T(8,128)S(1)} all-gather(f32[64,128]{1,0:T(8,128)S(1)} %get-tuple-element.11), channel_id=1, replica_groups=mesh['rows'=8,'hub'=4] {'rows'}, dimensions={0}, use_global_device_ids=true | all-gather | bytes 294912 | tf_op jit(solution)/shard_map/all_gather | solution.py:91
  127.3 9.2 %fusion.57 = f32[72,1,128]{2,1,0:T(1,128)S(1)} fusion(f32[72,128,1]{1,2,0:T(1,128)S(1)} %bitcast.111, f32[72,128,128]{2,1,0:T(8,128)} %param.15), kind=kOutput, calls=%fused_computation.104 | convolution fusion | flops 14155776 | bytes 4792320 | tf_op jit(solution)/shard_map/bij,bj->bi/dot_general | solution.py:93
  136.7 23.6 %psum.22 = f32[32,128]{1,0:T(8,128)S(1)} all-reduce(f32[32,128]{1,0:T(8,128)} %reduce-scatter.6.cloned.1.call-done), channel_id=1, replica_groups=mesh['rows'=8,'hub'=4] {'rows'}, use_global_device_ids=true, to_apply=%region_8.9 | all-reduce | flops 4096 | bytes 32768 | tf_op jit(solution)/shard_map/psum | solution.py:85
  160.3 13.4 %all_gather.21 = f32[128,128]{1,0:T(8,128)S(1)} all-gather(f32[32,128]{1,0:T(8,128)S(1)} %get-tuple-element.5), channel_id=1, replica_groups=mesh['rows'=8,'hub'=4] {'hub'}, dimensions={0}, use_global_device_ids=true | all-gather | bytes 81920 | tf_op jit(solution)/shard_map/all_gather | solution.py:90
  174.2 2.5 fusion.59
  178.1 5.8 %fusion.60 = f32[72,1,128]{2,1,0:T(1,128)S(1)} fusion(f32[72,128,1]{1,2,0:T(1,128)S(1)} %bitcast.107, f32[72,128,128]{2,1,0:T(8,128)} %param.15), kind=kOutput, calls=%fused_computation.107 | convolution fusion | flops 14155776 | bytes 4792320 | tf_op jit(solution)/shard_map/bij,bi->bj/dot_general | solution.py:61
  185.3 3.4 %all-to-all-start.3 = ((f32[8,27,128]{2,1,0:T(8,128)}), f32[8,27,128]{2,1,0:T(8,128)S(1)}, u32[]{:S(2)}, u32[]{:S(2)}) async-start(f32[8,27,128]{2,1,0:T(8,128)} %reshape.46), calls=%async_computation.5 | async-start | bytes 262144 | tf_op jit(solution)/shard_map/all_to_all | solution.py:63
  188.8 1.4 fusion.61
  191.0 3.2 %all-to-all-done.3 = f32[8,27,128]{2,1,0:T(8,128)S(1)} async-done(((f32[8,27,128]{2,1,0:T(8,128)}), f32[8,27,128]{2,1,0:T(8,128)S(1)}, u32[]{:S(2)}, u32[]{:S(2)}) %all-to-all-start.3) | async-done | bytes 110624 | tf_op jit(solution)/shard_map/all_to_all | solution.py:63
  195.1 8.3 %all_gather.22 = f32[512,128]{1,0:T(8,128)S(1)} all-gather(f32[64,128]{1,0:T(8,128)S(1)} %get-tuple-element.13), channel_id=1, replica_groups=mesh['rows'=8,'hub'=4] {'rows'}, dimensions={0}, use_global_device_ids=true | all-gather | bytes 294912 | tf_op jit(solution)/shard_map/all_gather | solution.py:91
  204.0 9.2 %fusion.62 = f32[72,1,128]{2,1,0:T(1,128)S(1)} fusion(f32[72,128,1]{1,2,0:T(1,128)S(1)} %bitcast.108, f32[72,128,128]{2,1,0:T(8,128)} %param.15), kind=kOutput, calls=%fused_computation.109 | convolution fusion | flops 14155776 | bytes 4792320 | tf_op jit(solution)/shard_map/bij,bj->bi/dot_general | solution.py:93
  213.3 23.6 %psum.23 = f32[32,128]{1,0:T(8,128)S(1)} all-reduce(f32[32,128]{1,0:T(8,128)} %reduce-scatter.8.cloned.1.call-done), channel_id=1, replica_groups=mesh['rows'=8,'hub'=4] {'rows'}, use_global_device_ids=true, to_apply=%region_11.12 | all-reduce | flops 4096 | bytes 32768 | tf_op jit(solution)/shard_map/psum | solution.py:85
  237.6 13.1 %all_gather.23 = f32[128,128]{1,0:T(8,128)S(1)} all-gather(f32[32,128]{1,0:T(8,128)S(1)} %get-tuple-element.3), channel_id=1, replica_groups=mesh['rows'=8,'hub'=4] {'hub'}, dimensions={0}, use_global_device_ids=true | all-gather | bytes 81920 | tf_op jit(solution)/shard_map/all_gather | solution.py:90
  251.2 2.5 fusion.63
  (83 shorter events, 22.4 us)
Async XLA Ops:
  7.2 11.3 %copy-start = (f32[24,128,128]{2,1,0:T(8,128)S(1)}, f32[24,128,128]{2,1,0:T(8,128)}, u32[]{:S(2)}) copy-start(f32[24,128,128]{2,1,0:T(8,128)} %param.19) | copy-start | bytes 4718596
  7.2 34.5 %copy-start.7 = (f32[64,128]{1,0:T(8,128)S(1)}, f32[64,128]{1,0:T(8,128)}, u32[]{:S(2)}) copy-start(f32[64,128]{1,0:T(8,128)} %param.22) | copy-start | bytes 98308
  7.2 34.5 %copy-start.3 = (f32[64,128]{1,0:T(8,128)S(1)}, f32[64,128]{1,0:T(8,128)}, u32[]{:S(2)}) copy-start(f32[64,128]{1,0:T(8,128)} %param.23) | copy-start | bytes 98308
  7.2 34.5 %copy-start.2 = (f32[64,128]{1,0:T(8,128)S(1)}, f32[64,128]{1,0:T(8,128)}, u32[]{:S(2)}) copy-start(f32[64,128]{1,0:T(8,128)} %param.24) | copy-start | bytes 98308
  11.3 20.7 %all-to-all-start = ((s32[8,1,27]{2,1,0:T(1,128)}), s32[8,1,27]{2,1,0:T(1,128)S(1)}, u32[]{:S(2)}, u32[]{:S(2)}) async-start(s32[8,1,27]{2,1,0:T(1,128)} %all_to_all.15), calls=%async_computation | async-start | bytes 8192 | tf_op jit(solution)/shard_map/all_to_all | solution.py:43
  16.5 43.7 %reduce-scatter.4.cloned.1.call-start = ((), (), s32[]{:S(2)}) async-start(), calls=%async_computation.7 | async-start | bytes 81920 | tf_op jit(solution)/shard_map/reduce_scatter | solution.py:84
  24.7 35.4 %copy-start.10 = (s32[72]{0:T(128)S(1)}, s32[72]{0:T(128)}, u32[]{:S(2)}) copy-start(s32[72]{0:T(128)} %param.16) | copy-start | bytes 868
  24.7 59.2 %copy-start.4 = (f32[32,128]{1,0:T(8,128)S(1)}, f32[32,128]{1,0:T(8,128)}, u32[]{:S(2)}) copy-start(f32[32,128]{1,0:T(8,128)} %param.27) | copy-start | bytes 49156
  24.7 59.2 %copy-start.5 = (f32[32,128]{1,0:T(8,128)S(1)}, f32[32,128]{1,0:T(8,128)}, u32[]{:S(2)}) copy-start(f32[32,128]{1,0:T(8,128)} %param.26) | copy-start | bytes 49156
  24.7 59.2 %copy-start.8 = (f32[32,128]{1,0:T(8,128)S(1)}, f32[32,128]{1,0:T(8,128)}, u32[]{:S(2)}) copy-start(f32[32,128]{1,0:T(8,128)} %param.25) | copy-start | bytes 49156
  30.5 70.1 %copy-start.1 = (f32[16,128]{1,0:T(8,128)S(1)}, f32[16,128]{1,0:T(8,128)}, u32[]{:S(2)}) copy-start(f32[16,128]{1,0:T(8,128)} %param.28) | copy-start | bytes 24580
  30.5 70.1 %copy-start.6 = (f32[16,128]{1,0:T(8,128)S(1)}, f32[16,128]{1,0:T(8,128)}, u32[]{:S(2)}) copy-start(f32[16,128]{1,0:T(8,128)} %param.29) | copy-start | bytes 24580
  30.5 70.2 %copy-start.11 = (s32[24]{0:T(128)S(1)}, s32[24]{0:T(128)}, u32[]{:S(2)}) copy-start(s32[24]{0:T(128)} %param.20) | copy-start | bytes 292
  32.0 9.7 %all-to-all-start.1 = ((f32[8,27,128]{2,1,0:T(8,128)}), f32[8,27,128]{2,1,0:T(8,128)S(1)}, u32[]{:S(2)}, u32[]{:S(2)}) async-start(f32[8,27,128]{2,1,0:T(8,128)} %reshape.42), calls=%async_computation.1 | async-start | bytes 262144 | tf_op jit(solution)/shard_map/all_to_all | solution.py:63
  60.2 53.9 %copy-start.9 = (s32[24]{0:T(128)S(1)}, s32[24]{0:T(128)}, u32[]{:S(2)}) copy-start(s32[24]{0:T(128)} %param.21) | copy-start | bytes 292
  109.2 8.9 %all-to-all-start.2 = ((f32[8,27,128]{2,1,0:T(8,128)}), f32[8,27,128]{2,1,0:T(8,128)S(1)}, u32[]{:S(2)}, u32[]{:S(2)}) async-start(f32[8,27,128]{2,1,0:T(8,128)} %reshape.44), calls=%async_computation.3 | async-start | bytes 262144 | tf_op jit(solution)/shard_map/all_to_all | solution.py:63
  112.7 24.0 %reduce-scatter.6.cloned.1.call-start = ((), (), s32[]{:S(2)}) async-start(), calls=%async_computation.8 | async-start | bytes 81920 | tf_op jit(solution)/shard_map/reduce_scatter | solution.py:84
  185.3 8.9 %all-to-all-start.3 = ((f32[8,27,128]{2,1,0:T(8,128)}), f32[8,27,128]{2,1,0:T(8,128)S(1)}, u32[]{:S(2)}, u32[]{:S(2)}) async-start(f32[8,27,128]{2,1,0:T(8,128)} %reshape.46), calls=%async_computation.5 | async-start | bytes 262144 | tf_op jit(solution)/shard_map/all_to_all | solution.py:63
  188.7 24.6 %reduce-scatter.8.cloned.1.call-start = ((), (), s32[]{:S(2)}) async-start(), calls=%async_computation.9 | async-start | bytes 81920 | tf_op jit(solution)/shard_map/reduce_scatter | solution.py:84
Sparse Core Ops, SparseCore 0:
  21.5 20.9 reduce-scatter.3
  115.7 20.7 reduce-scatter.5
  191.8 20.7 reduce-scatter.7
where the time goes:
time: 262 us; the launch traced here: 261 us
  blocking collectives  136 us (52%)
  matrix products  62.6 us (24%)
  starting transfers between devices  16.3 us (6%)
  local copies, waits for them, and re-layouts  15 us (6%)
  between operations  14 us (5%)
  waiting for transfers between devices  10.7 us (4%)
  other arithmetic  6.44 us (2%)
    psum x3, blocking collectives, on_device(): hub_sums = lax.psum(hub_sums, 'rows')  70.9 us
    all_gather x3, blocking collectives, on_device(): hub_full = lax.all_gather(hub_extra, 'hub', axis=0, tiled=True)  40.1 us
    dot_general x3, matrix products, on_device(): jnp.einsum('bij,bj->bi', tail_blocks, tail_picked, precision=highest)  27.6 us
    all_gather x3, blocking collectives, on_device(): gathered = lax.all_gather(tail_extra, 'rows', axis=0, tiled=True)  25 us
    dot_general x3, matrix products, on_device(): jnp.einsum('bij,bi->bj', tail_blocks, duals[tail_row], precision=highest)  17.4 us
    all_to_all x3, starting transfers between devices, on_device(): lax.all_to_all(outgoing.reshape(row_devs, capacity, width), 'rows', split...  11 us
    all_to_all x3, waiting for transfers between devices, on_device(): lax.all_to_all(outgoing.reshape(row_devs, capacity, width), 'rows', split...  10.6 us
    dot_general x3, matrix products, on_device(): jnp.einsum('bij,bj->bi', hub_blocks, hub_full[hub_col], precision=highest)  7.63 us
  transfers between devices with their start and end apart: 7, of which 3 were waited for; matrix products, arithmetic and copies ran while one was open for 20% of the time, Pallas kernels for 0%

commit v1 on v0

--- a/solution.py
+++ b/solution.py
@@ -82,7 +82,11 @@
             hub_pick, hub_terms, precision=highest, preferred_element_type=jnp.float32
         )
         hub_sums = lax.psum_scatter(hub_partial, "hub", scatter_dimension=0, tiled=True)
-        hub_sums = lax.psum(hub_sums, "rows")
+        hub_sums = hub_sums
+        for hop in (1, 2, 4):
+            hub_sums = hub_sums + lax.ppermute(
+                hub_sums, "rows", [(dev, dev ^ hop) for dev in range(8)]
+            )
         hub_next = jnp.minimum(
             jnp.maximum(hub_state - primal_step * (cost_hub - hub_sums), 0.0), upper_hub
         )

time: 262 us -> 244 us (0.931)
  blocking collectives: 136 us -> 67.7 us
  waiting for transfers between devices: 10.7 us -> 51.9 us
  starting transfers between devices: 16.3 us -> 22.5 us
    psum x3 -> x0, blocking collectives: 70.9 us -> none  [on_device(): hub_sums = lax.psum(hub_sums, 'rows')]
    reduce_scatter x3, waiting for transfers between devices: 0.01 us -> 32.2 us  [on_device(): lax.psum_scatter(hub_partial, 'hub', scatter_dimension=0, tiled=True)]
    ppermute x0 -> x9, waiting for transfers between devices: none -> 9.15 us  [on_device(): lax.ppermute(hub_sums, 'rows', [(dev, dev ^ hop) for dev in range(8)])]
    ppermute x0 -> x9, starting transfers between devices: none -> 6.28 us  [on_device(): lax.ppermute(hub_sums, 'rows', [(dev, dev ^ hop) for dev in range(8)])]
    all_gather x3, blocking collectives: 25 us -> 27.8 us  [on_device(): gathered = lax.all_gather(tail_extra, 'rows', axis=0, tiled=True)]
  transfers between devices with their start and end apart: 7 -> 16, of which waited for: 3 -> 9; matrix products, arithmetic and copies ran while one was open for 20% -> 21% of each run, Pallas kernels for 0% -> 0%
where the time goes in v1:
time: 244 us; the launch traced here: 242 us
  blocking collectives  67.7 us (28%)
  matrix products  62.5 us (26%)
  waiting for transfers between devices  51.9 us (21%)
  starting transfers between devices  22.5 us (9%)
  local copies, waits for them, and re-layouts  15.1 us (6%)
  between operations  14.1 us (6%)
  other arithmetic  8.66 us (4%)
    all_gather x3, blocking collectives, on_device(): hub_full = lax.all_gather(hub_extra, 'hub', axis=0, tiled=True)  39.9 us
    reduce_scatter x3, waiting for transfers between devices, on_device(): lax.psum_scatter(hub_partial, 'hub', scatter_dimension=0, tiled=True)  32.2 us
    all_gather x3, blocking collectives, on_device(): gathered = lax.all_gather(tail_extra, 'rows', axis=0, tiled=True)  27.8 us
    dot_general x3, matrix products, on_device(): jnp.einsum('bij,bj->bi', tail_blocks, tail_picked, precision=highest)  27.6 us
    dot_general x3, matrix products, on_device(): jnp.einsum('bij,bi->bj', tail_blocks, duals[tail_row], precision=highest)  17.4 us
    all_to_all x3, starting transfers between devices, on_device(): lax.all_to_all(outgoing.reshape(row_devs, capacity, width), 'rows', split...  10.9 us
    all_to_all x3, waiting for transfers between devices, on_device(): lax.all_to_all(outgoing.reshape(row_devs, capacity, width), 'rows', split...  10.5 us
    ppermute x9, waiting for transfers between devices, on_device(): lax.ppermute(hub_sums, 'rows', [(dev, dev ^ hop) for dev in range(8)])  9.15 us
  transfers between devices with their start and end apart: 16, of which 9 were waited for; matrix products, arithmetic and copies ran while one was open for 21% of the time, Pallas kernels for 0%

profile of v1, /device:TPU:0, one launch (start us, length us, event | category | flops | bytes accessed | tf_op | source)
XLA Modules:
  0.0 242.4 jit_solution(16396664872871633210)
XLA Ops:
  11.3 5.2 %all-to-all-start = ((s32[8,1,27]{2,1,0:T(1,128)}), s32[8,1,27]{2,1,0:T(1,128)S(1)}, u32[]{:S(2)}, u32[]{:S(2)}) async-start(s32[8,1,27]{2,1,0:T(1,128)} %all_to_all.15), calls=%async_computation | async-start | bytes 8192 | tf_op jit(solution)/shard_map/all_to_all | solution.py:43
  18.5 1.4 fusion.54
  19.9 1.5 fusion.26
  24.7 5.8 %fusion.52 = f32[72,1,128]{2,1,0:T(1,128)S(1)} fusion(f32[72,128,1]{1,2,0:T(1,128)S(1)} %bitcast.112, f32[72,128,128]{2,1,0:T(8,128)} %param.15), kind=kOutput, calls=%fused_computation.99 | convolution fusion | flops 14155776 | bytes 4792320 | tf_op jit(solution)/shard_map/bij,bi->bj/dot_general | solution.py:61
  32.0 4.2 %all-to-all-start.1 = ((f32[8,27,128]{2,1,0:T(8,128)}), f32[8,27,128]{2,1,0:T(8,128)S(1)}, u32[]{:S(2)}, u32[]{:S(2)}) async-start(f32[8,27,128]{2,1,0:T(8,128)} %reshape.42), calls=%async_computation.1 | async-start | bytes 262144 | tf_op jit(solution)/shard_map/all_to_all | solution.py:63
  37.4 4.2 %all-to-all-done.1 = f32[8,27,128]{2,1,0:T(8,128)S(1)} async-done(((f32[8,27,128]{2,1,0:T(8,128)}), f32[8,27,128]{2,1,0:T(8,128)S(1)}, u32[]{:S(2)}, u32[]{:S(2)}) %all-to-all-start.1) | async-done | bytes 110624 | tf_op jit(solution)/shard_map/all_to_all | solution.py:63
  42.5 9.2 %all_gather.18 = f32[512,128]{1,0:T(8,128)S(1)} all-gather(f32[64,128]{1,0:T(8,128)S(1)} %get-tuple-element.9), channel_id=1, replica_groups=mesh['rows'=8,'hub'=4] {'rows'}, dimensions={0}, use_global_device_ids=true | all-gather | bytes 294912 | tf_op jit(solution)/shard_map/all_gather | solution.py:95
  53.1 1.5 collective-permute-start.1
  54.6 9.2 %fusion.53 = f32[72,1,128]{2,1,0:T(1,128)S(1)} fusion(f32[72,128,1]{1,2,0:T(1,128)S(1)} %bitcast.108, f32[72,128,128]{2,1,0:T(8,128)} %param.15), kind=kOutput, calls=%fused_computation.100 | convolution fusion | flops 14155776 | bytes 4792320 | tf_op jit(solution)/shard_map/bij,bj->bi/dot_general | solution.py:97
  64.5 3.0 %collective-permute-done.2 = f32[32,128]{1,0:T(8,128)S(1)} collective-permute-done((f32[32,128]{1,0:T(8,128)S(1)}, f32[32,128]{1,0:T(8,128)S(1)}, u32[]{:S(2)}, u32[]{:S(2)}) %collective-permute-start.2) | collective-permute-done | bytes 16416 | tf_op jit(solution)/shard_map/ppermute | solution.py:87
  67.6 13.5 %all_gather.19 = f32[128,128]{1,0:T(8,128)S(1)} all-gather(f32[32,128]{1,0:T(8,128)S(1)} %get-tuple-element.7), channel_id=1, replica_groups=mesh['rows'=8,'hub'=4] {'hub'}, dimensions={0}, use_global_device_ids=true | all-gather | bytes 81920 | tf_op jit(solution)/shard_map/all_gather | solution.py:94
  81.7 2.5 %fusion.55 = f32[24,1,128]{2,1,0:T(1,128)S(1)} fusion(f32[24,128,1]{1,2,0:T(1,128)S(1)} %bitcast.117, f32[24,128,128]{2,1,0:T(8,128)S(1)} %copy-done), kind=kOutput, calls=%fused_computation.102 | convolution fusion | flops 4718592 | bytes 1597440 | tf_op jit(solution)/shard_map/bij,bj->bi/dot_general | solution.py:98
  85.5 5.8 %fusion.56 = f32[72,1,128]{2,1,0:T(1,128)S(1)} fusion(f32[72,128,1]{1,2,0:T(1,128)S(1)} %bitcast.111, f32[72,128,128]{2,1,0:T(8,128)} %param.15), kind=kOutput, calls=%fused_computation.103 | convolution fusion | flops 14155776 | bytes 4792320 | tf_op jit(solution)/shard_map/bij,bi->bj/dot_general | solution.py:61
  92.8 3.4 %all-to-all-start.2 = ((f32[8,27,128]{2,1,0:T(8,128)}), f32[8,27,128]{2,1,0:T(8,128)S(1)}, u32[]{:S(2)}, u32[]{:S(2)}) async-start(f32[8,27,128]{2,1,0:T(8,128)} %reshape.44), calls=%async_computation.3 | async-start | bytes 262144 | tf_op jit(solution)/shard_map/all_to_all | solution.py:63
  98.5 3.1 %all-to-all-done.2 = f32[8,27,128]{2,1,0:T(8,128)S(1)} async-done(((f32[8,27,128]{2,1,0:T(8,128)}), f32[8,27,128]{2,1,0:T(8,128)S(1)}, u32[]{:S(2)}, u32[]{:S(2)}) %all-to-all-start.2) | async-done | bytes 110624 | tf_op jit(solution)/shard_map/all_to_all | solution.py:63
  101.8 16.8 %reduce-scatter.6.cloned.1.call-done = f32[32,128]{1,0:T(8,128)} async-done(((f32[128,128]{1,0:T(8,128)}), f32[32,128]{1,0:T(8,128)}) %reduce-scatter.6.cloned.1.call-update) | async-done | bytes 16400 | tf_op jit(solution)/shard_map/reduce_scatter | solution.py:84
  118.6 9.3 %all_gather.20 = f32[512,128]{1,0:T(8,128)S(1)} all-gather(f32[64,128]{1,0:T(8,128)S(1)} %get-tuple-element.11), channel_id=1, replica_groups=mesh['rows'=8,'hub'=4] {'rows'}, dimensions={0}, use_global_device_ids=true | all-gather | bytes 294912 | tf_op jit(solution)/shard_map/all_gather | solution.py:95
  129.2 1.5 collective-permute-start.4
  130.7 9.2 %fusion.57 = f32[72,1,128]{2,1,0:T(1,128)S(1)} fusion(f32[72,128,1]{1,2,0:T(1,128)S(1)} %bitcast.109, f32[72,128,128]{2,1,0:T(8,128)} %param.15), kind=kOutput, calls=%fused_computation.104 | convolution fusion | flops 14155776 | bytes 4792320 | tf_op jit(solution)/shard_map/bij,bj->bi/dot_general | solution.py:97
  140.7 3.1 %collective-permute-done.5 = f32[32,128]{1,0:T(8,128)S(1)} collective-permute-done((f32[32,128]{1,0:T(8,128)S(1)}, f32[32,128]{1,0:T(8,128)S(1)}, u32[]{:S(2)}, u32[]{:S(2)}) %collective-permute-start.5) | collective-permute-done | bytes 16416 | tf_op jit(solution)/shard_map/ppermute | solution.py:87
  143.8 13.3 %all_gather.21 = f32[128,128]{1,0:T(8,128)S(1)} all-gather(f32[32,128]{1,0:T(8,128)S(1)} %get-tuple-element.5), channel_id=1, replica_groups=mesh['rows'=8,'hub'=4] {'hub'}, dimensions={0}, use_global_device_ids=true | all-gather | bytes 81920 | tf_op jit(solution)/shard_map/all_gather | solution.py:94
  157.7 2.5 %fusion.59 = f32[24,1,128]{2,1,0:T(1,128)S(1)} fusion(f32[24,128,1]{1,2,0:T(1,128)S(1)} %bitcast.119, f32[24,128,128]{2,1,0:T(8,128)S(1)} %copy-done), kind=kOutput, calls=%fused_computation.106 | convolution fusion | flops 4718592 | bytes 1597440 | tf_op jit(solution)/shard_map/bij,bj->bi/dot_general | solution.py:98
  161.5 5.8 %fusion.60 = f32[72,1,128]{2,1,0:T(1,128)S(1)} fusion(f32[72,128,1]{1,2,0:T(1,128)S(1)} %bitcast.110, f32[72,128,128]{2,1,0:T(8,128)} %param.15), kind=kOutput, calls=%fused_computation.107 | convolution fusion | flops 14155776 | bytes 4792320 | tf_op jit(solution)/shard_map/bij,bi->bj/dot_general | solution.py:61
  168.8 3.4 %all-to-all-start.3 = ((f32[8,27,128]{2,1,0:T(8,128)}), f32[8,27,128]{2,1,0:T(8,128)S(1)}, u32[]{:S(2)}, u32[]{:S(2)}) async-start(f32[8,27,128]{2,1,0:T(8,128)} %reshape.46), calls=%async_computation.5 | async-start | bytes 262144 | tf_op jit(solution)/shard_map/all_to_all | solution.py:63
  174.5 3.1 %all-to-all-done.3 = f32[8,27,128]{2,1,0:T(8,128)S(1)} async-done(((f32[8,27,128]{2,1,0:T(8,128)}), f32[8,27,128]{2,1,0:T(8,128)S(1)}, u32[]{:S(2)}, u32[]{:S(2)}) %all-to-all-start.3) | async-done | bytes 110624 | tf_op jit(solution)/shard_map/all_to_all | solution.py:63
  178.4 14.7 %reduce-scatter.8.cloned.1.call-done = f32[32,128]{1,0:T(8,128)} async-done(((f32[128,128]{1,0:T(8,128)}), f32[32,128]{1,0:T(8,128)}) %reduce-scatter.8.cloned.1.call-update) | async-done | bytes 16400 | tf_op jit(solution)/shard_map/reduce_scatter | solution.py:84
  193.2 9.3 %all_gather.22 = f32[512,128]{1,0:T(8,128)S(1)} all-gather(f32[64,128]{1,0:T(8,128)S(1)} %get-tuple-element.13), channel_id=1, replica_groups=mesh['rows'=8,'hub'=4] {'rows'}, dimensions={0}, use_global_device_ids=true | all-gather | bytes 294912 | tf_op jit(solution)/shard_map/all_gather | solution.py:95
  203.8 1.4 collective-permute-start.7
  205.2 9.2 %fusion.62 = f32[72,1,128]{2,1,0:T(1,128)S(1)} fusion(f32[72,128,1]{1,2,0:T(1,128)S(1)} %bitcast.107, f32[72,128,128]{2,1,0:T(8,128)} %param.15), kind=kOutput, calls=%fused_computation.109 | convolution fusion | flops 14155776 | bytes 4792320 | tf_op jit(solution)/shard_map/bij,bj->bi/dot_general | solution.py:97
  215.2 3.0 %collective-permute-done.8 = f32[32,128]{1,0:T(8,128)S(1)} collective-permute-done((f32[32,128]{1,0:T(8,128)S(1)}, f32[32,128]{1,0:T(8,128)S(1)}, u32[]{:S(2)}, u32[]{:S(2)}) %collective-permute-start.8) | collective-permute-done | bytes 16416 | tf_op jit(solution)/shard_map/ppermute | solution.py:87
  218.8 13.1 %all_gather.23 = f32[128,128]{1,0:T(8,128)S(1)} all-gather(f32[32,128]{1,0:T(8,128)S(1)} %get-tuple-element.3), channel_id=1, replica_groups=mesh['rows'=8,'hub'=4] {'hub'}, dimensions={0}, use_global_device_ids=true | all-gather | bytes 81920 | tf_op jit(solution)/shard_map/all_gather | solution.py:94
  232.5 2.5 %fusion.63 = f32[24,1,128]{2,1,0:T(1,128)S(1)} fusion(f32[24,128,1]{1,2,0:T(1,128)S(1)} %bitcast.115, f32[24,128,128]{2,1,0:T(8,128)S(1)} %copy-done), kind=kOutput, calls=%fused_computation.110 | convolution fusion | flops 4718592 | bytes 1597440 | tf_op jit(solution)/shard_map/bij,bj->bi/dot_general | solution.py:98
  (104 shorter events, 33.5 us)
Async XLA Ops:
  7.2 11.3 %copy-start = (f32[24,128,128]{2,1,0:T(8,128)S(1)}, f32[24,128,128]{2,1,0:T(8,128)}, u32[]{:S(2)}) copy-start(f32[24,128,128]{2,1,0:T(8,128)} %param.19) | copy-start | bytes 4718596
  7.2 34.5 %copy-start.7 = (f32[64,128]{1,0:T(8,128)S(1)}, f32[64,128]{1,0:T(8,128)}, u32[]{:S(2)}) copy-start(f32[64,128]{1,0:T(8,128)} %param.22) | copy-start | bytes 98308
  7.2 34.5 %copy-start.2 = (f32[64,128]{1,0:T(8,128)S(1)}, f32[64,128]{1,0:T(8,128)}, u32[]{:S(2)}) copy-start(f32[64,128]{1,0:T(8,128)} %param.24) | copy-start | bytes 98308
  7.2 34.5 %copy-start.3 = (f32[64,128]{1,0:T(8,128)S(1)}, f32[64,128]{1,0:T(8,128)}, u32[]{:S(2)}) copy-start(f32[64,128]{1,0:T(8,128)} %param.23) | copy-start | bytes 98308
  11.3 20.7 %all-to-all-start = ((s32[8,1,27]{2,1,0:T(1,128)}), s32[8,1,27]{2,1,0:T(1,128)S(1)}, u32[]{:S(2)}, u32[]{:S(2)}) async-start(s32[8,1,27]{2,1,0:T(1,128)} %all_to_all.15), calls=%async_computation | async-start | bytes 8192 | tf_op jit(solution)/shard_map/all_to_all | solution.py:43
  16.5 26.0 %reduce-scatter.4.cloned.1.call-start = ((), (), s32[]{:S(2)}) async-start(), calls=%async_computation.7 | async-start | bytes 81920 | tf_op jit(solution)/shard_map/reduce_scatter | solution.py:84
  24.7 39.7 %copy-start.10 = (s32[72]{0:T(128)S(1)}, s32[72]{0:T(128)}, u32[]{:S(2)}) copy-start(s32[72]{0:T(128)} %param.16) | copy-start | bytes 868
  24.7 42.9 %copy-start.4 = (f32[32,128]{1,0:T(8,128)S(1)}, f32[32,128]{1,0:T(8,128)}, u32[]{:S(2)}) copy-start(f32[32,128]{1,0:T(8,128)} %param.27) | copy-start | bytes 49156
  24.7 42.9 %copy-start.5 = (f32[32,128]{1,0:T(8,128)S(1)}, f32[32,128]{1,0:T(8,128)}, u32[]{:S(2)}) copy-start(f32[32,128]{1,0:T(8,128)} %param.26) | copy-start | bytes 49156
  24.7 42.9 %copy-start.8 = (f32[32,128]{1,0:T(8,128)S(1)}, f32[32,128]{1,0:T(8,128)}, u32[]{:S(2)}) copy-start(f32[32,128]{1,0:T(8,128)} %param.25) | copy-start | bytes 49156
  30.5 53.7 %copy-start.1 = (f32[16,128]{1,0:T(8,128)S(1)}, f32[16,128]{1,0:T(8,128)}, u32[]{:S(2)}) copy-start(f32[16,128]{1,0:T(8,128)} %param.28) | copy-start | bytes 24580
  30.5 53.7 %copy-start.6 = (f32[16,128]{1,0:T(8,128)S(1)}, f32[16,128]{1,0:T(8,128)}, u32[]{:S(2)}) copy-start(f32[16,128]{1,0:T(8,128)} %param.29) | copy-start | bytes 24580
  30.5 53.7 %copy-start.11 = (s32[24]{0:T(128)S(1)}, s32[24]{0:T(128)}, u32[]{:S(2)}) copy-start(s32[24]{0:T(128)} %param.20) | copy-start | bytes 292
  32.0 9.7 %all-to-all-start.1 = ((f32[8,27,128]{2,1,0:T(8,128)}), f32[8,27,128]{2,1,0:T(8,128)S(1)}, u32[]{:S(2)}, u32[]{:S(2)}) async-start(f32[8,27,128]{2,1,0:T(8,128)} %reshape.42), calls=%async_computation.1 | async-start | bytes 262144 | tf_op jit(solution)/shard_map/all_to_all | solution.py:63
  42.5 9.8 %collective-permute-start = (f32[32,128]{1,0:T(8,128)}, f32[32,128]{1,0:T(8,128)S(1)}, u32[]{:S(2)}, u32[]{:S(2)}) collective-permute-start(f32[32,128]{1,0:T(8,128)} %reduce-scatter.4.cloned.1.call-done), channel_id=1, source_target_pairs={{0,4},{4,0},{8,12},{12,8},{16,20},{20,16},{24,28},{28,24},{1,5},{5... | collective-permute-start | bytes 49160 | tf_op jit(solution)/shard_map/ppermute | solution.py:87
  53.1 10.7 %collective-permute-start.1 = (f32[32,128]{1,0:T(8,128)S(1)}, f32[32,128]{1,0:T(8,128)S(1)}, u32[]{:S(2)}, u32[]{:S(2)}) collective-permute-start(f32[32,128]{1,0:T(8,128)S(1)} %add.102), channel_id=1, source_target_pairs={{0,8},{4,12},{8,0},{12,4},{16,24},{20,28},{24,16},{28,20},{1,9},{5... | collective-permute-start | bytes 49160 | tf_op jit(solution)/shard_map/ppermute | solution.py:87
  63.8 3.8 %collective-permute-start.2 = (f32[32,128]{1,0:T(8,128)S(1)}, f32[32,128]{1,0:T(8,128)S(1)}, u32[]{:S(2)}, u32[]{:S(2)}) collective-permute-start(f32[32,128]{1,0:T(8,128)S(1)} %add.103), channel_id=1, source_target_pairs={{0,16},{4,20},{8,24},{12,28},{16,0},{20,4},{24,8},{28,12},{1,17},{... | collective-permute-start | bytes 49160 | tf_op jit(solution)/shard_map/ppermute | solution.py:87
  64.4 33.2 %copy-start.9 = (s32[24]{0:T(128)S(1)}, s32[24]{0:T(128)}, u32[]{:S(2)}) copy-start(s32[24]{0:T(128)} %param.21) | copy-start | bytes 292
  92.8 8.8 %all-to-all-start.2 = ((f32[8,27,128]{2,1,0:T(8,128)}), f32[8,27,128]{2,1,0:T(8,128)S(1)}, u32[]{:S(2)}, u32[]{:S(2)}) async-start(f32[8,27,128]{2,1,0:T(8,128)} %reshape.44), calls=%async_computation.3 | async-start | bytes 262144 | tf_op jit(solution)/shard_map/all_to_all | solution.py:63
  96.2 22.4 %reduce-scatter.6.cloned.1.call-start = ((), (), s32[]{:S(2)}) async-start(), calls=%async_computation.8 | async-start | bytes 81920 | tf_op jit(solution)/shard_map/reduce_scatter | solution.py:84
  118.6 9.9 %collective-permute-start.3 = (f32[32,128]{1,0:T(8,128)}, f32[32,128]{1,0:T(8,128)S(1)}, u32[]{:S(2)}, u32[]{:S(2)}) collective-permute-start(f32[32,128]{1,0:T(8,128)} %reduce-scatter.6.cloned.1.call-done), channel_id=1, source_target_pairs={{0,4},{4,0},{8,12},{12,8},{16,20},{20,16},{24,28},{28,24},{1,5},{5... | collective-permute-start | bytes 49160 | tf_op jit(solution)/shard_map/ppermute | solution.py:87
  129.2 10.7 %collective-permute-start.4 = (f32[32,128]{1,0:T(8,128)S(1)}, f32[32,128]{1,0:T(8,128)S(1)}, u32[]{:S(2)}, u32[]{:S(2)}) collective-permute-start(f32[32,128]{1,0:T(8,128)S(1)} %add.108), channel_id=1, source_target_pairs={{0,8},{4,12},{8,0},{12,4},{16,24},{20,28},{24,16},{28,20},{1,9},{5... | collective-permute-start | bytes 49160 | tf_op jit(solution)/shard_map/ppermute | solution.py:87
  139.9 3.8 %collective-permute-start.5 = (f32[32,128]{1,0:T(8,128)S(1)}, f32[32,128]{1,0:T(8,128)S(1)}, u32[]{:S(2)}, u32[]{:S(2)}) collective-permute-start(f32[32,128]{1,0:T(8,128)S(1)} %add.109), channel_id=1, source_target_pairs={{0,16},{4,20},{8,24},{12,28},{16,0},{20,4},{24,8},{28,12},{1,17},{... | collective-permute-start | bytes 49160 | tf_op jit(solution)/shard_map/ppermute | solution.py:87
  168.8 8.8 %all-to-all-start.3 = ((f32[8,27,128]{2,1,0:T(8,128)}), f32[8,27,128]{2,1,0:T(8,128)S(1)}, u32[]{:S(2)}, u32[]{:S(2)}) async-start(f32[8,27,128]{2,1,0:T(8,128)} %reshape.46), calls=%async_computation.5 | async-start | bytes 262144 | tf_op jit(solution)/shard_map/all_to_all | solution.py:63
  172.2 21.0 %reduce-scatter.8.cloned.1.call-start = ((), (), s32[]{:S(2)}) async-start(), calls=%async_computation.9 | async-start | bytes 81920 | tf_op jit(solution)/shard_map/reduce_scatter | solution.py:84
  193.2 9.9 %collective-permute-start.6 = (f32[32,128]{1,0:T(8,128)}, f32[32,128]{1,0:T(8,128)S(1)}, u32[]{:S(2)}, u32[]{:S(2)}) collective-permute-start(f32[32,128]{1,0:T(8,128)} %reduce-scatter.8.cloned.1.call-done), channel_id=1, source_target_pairs={{0,4},{4,0},{8,12},{12,8},{16,20},{20,16},{24,28},{28,24},{1,5},{5... | collective-permute-start | bytes 49160 | tf_op jit(solution)/shard_map/ppermute | solution.py:87
  203.8 10.6 %collective-permute-start.7 = (f32[32,128]{1,0:T(8,128)S(1)}, f32[32,128]{1,0:T(8,128)S(1)}, u32[]{:S(2)}, u32[]{:S(2)}) collective-permute-start(f32[32,128]{1,0:T(8,128)S(1)} %add.113), channel_id=1, source_target_pairs={{0,8},{4,12},{8,0},{12,4},{16,24},{20,28},{24,16},{28,20},{1,9},{5... | collective-permute-start | bytes 49160 | tf_op jit(solution)/shard_map/ppermute | solution.py:87
  214.4 3.8 %collective-permute-start.8 = (f32[32,128]{1,0:T(8,128)S(1)}, f32[32,128]{1,0:T(8,128)S(1)}, u32[]{:S(2)}, u32[]{:S(2)}) collective-permute-start(f32[32,128]{1,0:T(8,128)S(1)} %add.114), channel_id=1, source_target_pairs={{0,16},{4,20},{8,24},{12,28},{16,0},{20,4},{24,8},{28,12},{1,17},{... | collective-permute-start | bytes 49160 | tf_op jit(solution)/shard_map/ppermute | solution.py:87
Sparse Core Ops, SparseCore 0:
  21.5 20.9 reduce-scatter.3
  99.2 19.3 reduce-scatter.5
  175.2 17.9 reduce-scatter.7
